TPU v7x, 512 devices: a whole 4x8x8 slice. The times are simulated.
512 devices in a mesh: dp: 32 (over x, y), tensor: 16 (over z, core).
Axes of the slice: x: 4, y: 8, z: 8, core: 2. Of those that a mesh axis runs over, the one named last changes fastest.
Arguments:
- queries: bfloat16 [4096, 16384], P('dp', 'tensor'), may hold values from -24 to 24
- draft_keys: bfloat16 [4096, 1024], P('dp'), may hold values from -6 to 6
- draft_values: bfloat16 [4096, 1024], P('dp'), may hold values from -6 to 6
- cache_keys: bfloat16 [64, 2048, 1024], P('dp', 'tensor'), may hold values from -24 to 24
- cache_values: bfloat16 [64, 2048, 1024], P('dp', 'tensor'), may hold values from -6 to 6
- out_weight: bfloat16 [16384, 16384], P('tensor', 'dp'), may hold values from -0.25 to 0.25
- cache_lengths: int32 [64], P('dp'), may hold values from 512 to 2048
- draft_lengths: int32 [64], replicated, may hold values from 8 to 64
- dest_group: int32 [64], replicated, may hold values from 0 to 31, as said below
- dest_offset: int32 [64], replicated, may hold values from 0 to 32, as said below
Outputs:
- verified: bfloat16 [3072, 16384], P('tensor', 'dp')
Inputs may be any that keep to these rules, and one draw needn't show every extreme that they name: `dest_group`: at most one request of a group has another group as destination, and each group receives at most one such request. `dest_offset`: blocks with the same destination never intersect and end at packed row 96 or before; a block moved to another group starts right after that group's own rows; in every draw some group's blocks fill all 96 rows.
All inputs are finite; a program needn't handle non-finite values.
Results may differ from a plain program's by a relative error of at most 0.017.
Values may be sent and summed in bfloat16 or wider, within the bound.
No kernel may reach another device: no remote copies, remote signals or barrier semaphores. Data moves between devices by JAX's collectives and lax.ppermute only.
A program may use at most 64 MiB of HBM per device.

v0:
```python
import jax
import jax.numpy as jnp
from jax import lax
from jax.sharding import PartitionSpec as P

HEADS = 128
KV_HEADS = 8
HEAD_DIM = 128
DRAFT = 64
GROUP_REQ = 2
PACK = 96
NEG_FILL = -1e30


def packed_sources(row_ids, draft_lengths, dest_group, dest_offset):
    request_ids = jnp.arange(dest_group.shape[0], dtype=jnp.int32)
    slot_group = row_ids // PACK
    slot_index = row_ids % PACK
    inside = (
        (dest_group[None, :] == slot_group[:, None])
        & (slot_index[:, None] >= dest_offset[None, :])
        & (slot_index[:, None] < (dest_offset + draft_lengths)[None, :])
    )
    request = jnp.sum(jnp.where(inside, request_ids[None, :], 0), axis=1)
    first_slot = jnp.sum(jnp.where(inside, dest_offset[None, :], 0), axis=1)
    return (request, slot_index - first_slot, jnp.any(inside, axis=1))


def attend_one(operands):
    queries_one, cache_k, cache_v, draft_k, draft_v, cache_len, draft_len = operands
    score_scale = HEAD_DIM ** (-0.5)
    cache_scores = (
        jnp.einsum("qkgd,lkd->kgql", queries_one, cache_k, preferred_element_type=jnp.float32)
        * score_scale
    )
    draft_scores = (
        jnp.einsum("qkgd,jkd->kgqj", queries_one, draft_k, preferred_element_type=jnp.float32)
        * score_scale
    )
    cache_pos = jnp.arange(cache_k.shape[0], dtype=jnp.int32)
    draft_pos = jnp.arange(draft_k.shape[0], dtype=jnp.int32)
    keep_cache = cache_pos < cache_len
    keep_draft = (draft_pos[None, :] <= draft_pos[:, None]) & (draft_pos[None, :] < draft_len)
    cache_scores = jnp.where(keep_cache, cache_scores, NEG_FILL)
    draft_scores = jnp.where(keep_draft, draft_scores, NEG_FILL)
    highest = jnp.maximum(
        jnp.max(cache_scores, axis=-1, keepdims=True), jnp.max(draft_scores, axis=-1, keepdims=True)
    )
    cache_exp = jnp.exp(cache_scores - highest)
    draft_exp = jnp.exp(draft_scores - highest)
    denominator = jnp.sum(cache_exp, axis=-1, keepdims=True) + jnp.sum(
        draft_exp, axis=-1, keepdims=True
    )
    cache_weights = (cache_exp / denominator).astype(jnp.bfloat16)
    draft_weights = (draft_exp / denominator).astype(jnp.bfloat16)
    mixed = jnp.einsum("kgql,lkd->qkgd", cache_weights, cache_v, preferred_element_type=jnp.float32)
    mixed = mixed + jnp.einsum(
        "kgqj,jkd->qkgd", draft_weights, draft_v, preferred_element_type=jnp.float32
    )
    is_live = draft_pos < draft_len
    return jnp.where(is_live[:, None, None, None], mixed, 0.0).astype(jnp.bfloat16)


def body(
    queries,
    draft_keys,
    draft_values,
    cache_keys,
    cache_values,
    out_weight,
    cache_lengths,
    draft_lengths,
    dest_group,
    dest_offset,
):
    tensor_count = lax.axis_size("tensor")
    data_count = lax.axis_size("dp")
    my_rank = lax.axis_index("tensor")
    my_group = lax.axis_index("dp")
    local_heads = HEADS // tensor_count
    group_heads = HEADS // KV_HEADS
    kv_local = max(1, local_heads // group_heads)
    per_kv = local_heads // kv_local
    kv_width = kv_local * HEAD_DIM
    span_rows = cache_keys.shape[1]
    copies = tensor_count // KV_HEADS

    def spread(cache_block):
        return jnp.repeat(
            cache_block.reshape(GROUP_REQ, span_rows, KV_HEADS, HEAD_DIM), copies, axis=2
        )

    full_keys, full_values = (
        lax.all_to_all(spread(cache_keys), "tensor", split_axis=2, concat_axis=1, tiled=True),
        lax.all_to_all(spread(cache_values), "tensor", split_axis=2, concat_axis=1, tiled=True),
    )
    kv_first = my_rank * local_heads // group_heads
    draft_k = lax.dynamic_slice_in_dim(draft_keys, kv_first * HEAD_DIM, kv_width, 1).reshape(
        GROUP_REQ, DRAFT, kv_local, HEAD_DIM
    )
    draft_v = lax.dynamic_slice_in_dim(draft_values, kv_first * HEAD_DIM, kv_width, 1).reshape(
        GROUP_REQ, DRAFT, kv_local, HEAD_DIM
    )
    local_queries = queries.reshape(GROUP_REQ, DRAFT, kv_local, per_kv, HEAD_DIM)
    my_lengths = lax.dynamic_slice_in_dim(draft_lengths, my_group * GROUP_REQ, GROUP_REQ)
    attended = lax.map(
        attend_one,
        (local_queries, full_keys, full_values, draft_k, draft_v, cache_lengths, my_lengths),
    )
    width_local = local_heads * HEAD_DIM
    attended_rows = attended.reshape(GROUP_REQ * DRAFT, width_local)
    target_rows = PACK * data_count // tensor_count
    home_all = lax.all_gather(attended_rows, "dp", axis=0, tiled=True)
    row_ids = jnp.arange(lax.axis_size("tensor") * target_rows, dtype=jnp.int32)
    request, within, is_live = packed_sources(row_ids, draft_lengths, dest_group, dest_offset)
    picked = jnp.take(home_all, request * DRAFT + within, axis=0)
    picked = jnp.where(is_live[:, None], picked, jnp.zeros((), jnp.bfloat16))
    return lax.psum_scatter(
        jnp.dot(picked, out_weight, preferred_element_type=jnp.float32).astype(jnp.bfloat16),
        "tensor",
        scatter_dimension=0,
        tiled=True,
    )


def solution(mesh):
    in_specs = (
        P("dp", "tensor"),
        P("dp", None),
        P("dp", None),
        P("dp", "tensor", None),
        P("dp", "tensor", None),
        P("tensor", "dp"),
        P("dp"),
        P(),
        P(),
        P(),
    )
    out_specs = P("tensor", "dp")
    return jax.shard_map(body, mesh=mesh, in_specs=in_specs, out_specs=out_specs, check_vma=False)
```

profile of v0, /device:TPU:8, one launch (start us, length us, event | category | flops | bytes accessed | tf_op | source)
XLA Modules:
  0.0 296.0 jit_solution(7023909836648568548)
XLA Ops:
  6.5 1.3 copy_bitcast_fusion.3
  7.9 1.2 broadcast_in_dim.102
  9.1 10.4 %all-to-all-start.1 = ((bf16[2,128,16,128]{3,1,0,2:T(8,128)(2,1)}), bf16[2,128,16,128]{3,1,0,2:T(8,128)(2,1)S(1)}, u32[]{:S(2)}, u32[]{:S(2)}) async-start(bf16[2,128,16,128]{3,1,0,2:T(8,128)(2,1)} %bitcast.25), calls=%async_computation.1 | async-start | bytes 2097152 | tf_op jit(solution)/shard_map/all_to_all | solution.py:94
  19.7 26.3 %all-to-all-done.1 = bf16[2,128,16,128]{3,1,0,2:T(8,128)(2,1)S(1)} async-done(((bf16[2,128,16,128]{3,1,0,2:T(8,128)(2,1)}), bf16[2,128,16,128]{3,1,0,2:T(8,128)(2,1)S(1)}, u32[]{:S(2)}, u32[]{:S(2)}) %all-to-all-start.1) | async-done | bytes 1048608 | tf_op jit(solution)/shard_map/all_to_all | solution.py:94
  46.0 1.3 broadcast_in_dim.101
  47.3 5.0 %all-to-all-start = ((bf16[2,128,16,128]{3,1,0,2:T(8,128)(2,1)}), bf16[2,128,16,128]{3,1,0,2:T(8,128)(2,1)}, u32[]{:S(2)}, u32[]{:S(2)}) async-start(bf16[2,128,16,128]{3,1,0,2:T(8,128)(2,1)} %bitcast.20), calls=%async_computation | async-start | bytes 2097152 | tf_op jit(solution)/shard_map/all_to_all | solution.py:95
  52.5 0.8 constant_dynamic-slice_fusion.1
  53.4 25.4 %all-to-all-done = bf16[2,128,16,128]{3,1,0,2:T(8,128)(2,1)} async-done(((bf16[2,128,16,128]{3,1,0,2:T(8,128)(2,1)}), bf16[2,128,16,128]{3,1,0,2:T(8,128)(2,1)}, u32[]{:S(2)}, u32[]{:S(2)}) %all-to-all-start) | async-done | bytes 1048608 | tf_op jit(solution)/shard_map/all_to_all | solution.py:95
  78.8 1.3 copy.36
  80.1 14.2 %while.10 = (s32[]{:T(128)}, bf16[2,64,1,8,128]{4,3,1,0,2:T(8,128)(2,1)}, s32[2]{0:T(128)S(1)}, bf16[2,2048,1,128]{3,1,2,0:T(8,128)(2,1)S(1)}, s32[2]{0:T(128)S(...) while((s32[]{:T(128)}, ...), condition=%wide.region_8.9_spmd, body=%wide.region_3.8_spmd.sunk | while | flops 566699072 | bytes 15692581 | solution.py:106
  83.2 0.9 bitcast_reduce_fusion.2
  84.2 0.9 fusion.71
  85.1 1.1 fusion.73
  86.5 0.7 copy_dynamic-update-slice_fusion.2
  89.3 0.7 iota_compare_fusion.5
  90.3 0.9 bitcast_reduce_fusion.2
  91.3 0.9 fusion.71
  92.2 1.1 fusion.73
  93.6 0.7 copy_dynamic-update-slice_fusion.2
  94.3 1.7 copy.62
  97.0 99.9 %all-gather.2.cloned.1.call-done = bf16[4096,1024]{1,0:T(8,128)(2,1)} async-done(((bf16[128,1024]{1,0:T(8,128)(2,1)}), bf16[4096,1024]{1,0:T(8,128)(2,1)}) %all-gather.2.cloned.1.call-update) | async-done | bytes 8388624 | tf_op jit(solution)/shard_map/all_gather | solution.py:113
  196.9 20.4 %gather_fusion = bf16[3072,1024]{1,0:T(8,128)(2,1)} fusion(bf16[4096,1024]{1,0:T(8,128)(2,1)} %all-gather.2.cloned.1.call-done, s32[3072]{0:T(1024)S(1)} %broadcast_clamp_fusion), kind=kCustom, calls=%fused_computation | custom fusion | bytes 12595200 | tf_op jit(solution)/shard_map/jit(_take)/gather | solution.py:116
  217.3 7.6 %fusion.34 = bf16[3072,512]{1,0:T(8,128)(2,1)} fusion(bf16[1024,512]{1,0:T(8,128)(2,1)S(1)} %copy-done, bf16[3072,1024]{1,0:T(8,128)(2,1)} %gather_fusion, pred[3072]{0:T(1024)(128)(4,1)S(1)} %compare_and_fusion.1, pred[3072]{0:T(1024)(128)(4,1)S(1)} %fusion.50), kind=kOutput, calls=%fused_computation.49 | convolution fusion | flops 3229089792 | bytes 10491904 | tf_op jit(solution)/shard_map/dot_general | solution.py:119
  224.9 64.2 %reduce-scatter.2.cloned.1.call-done = bf16[192,512]{1,0:T(8,128)(2,1)} async-done(((bf16[3072,512]{1,0:T(8,128)(2,1)}), bf16[192,512]{1,0:T(8,128)(2,1)}) %reduce-scatter.2.cloned.1.call-update) | async-done | bytes 196624 | tf_op jit(solution)/shard_map/reduce_scatter | solution.py:118
  (52 shorter events, 7.4 us)
Async XLA Ops:
  6.5 210.7 %copy-start = (bf16[1024,512]{1,0:T(8,128)(2,1)S(1)}, bf16[1024,512]{1,0:T(8,128)(2,1)}, u32[]{:S(2)}) copy-start(bf16[1024,512]{1,0:T(8,128)(2,1)} %param.17) | copy-start | bytes 3145732
  6.5 13.0 %copy-start.1 = (bf16[2,128,1024]{2,1,0:T(8,128)(2,1)S(1)}, bf16[2,128,1024]{2,1,0:T(8,128)(2,1)}, u32[]{:S(2)}) copy-start(bf16[2,128,1024]{2,1,0:T(8,128)(2,1)} %param.16) | copy-start | bytes 1572868
  7.8 44.5 %copy-start.2 = (bf16[128,1024]{1,0:T(8,128)(2,1)S(1)}, bf16[128,1024]{1,0:T(8,128)(2,1)}, u32[]{:S(2)}) copy-start(bf16[128,1024]{1,0:T(8,128)(2,1)} %param.12) | copy-start | bytes 786436
  7.8 44.6 %copy-start.6 = (s32[64]{0:T(128)S(1)}, s32[64]{0:T(128)}, u32[]{:S(2)}) copy-start(s32[64]{0:T(128)} %param.19) | copy-start | bytes 772
  9.1 36.9 %all-to-all-start.1 = ((bf16[2,128,16,128]{3,1,0,2:T(8,128)(2,1)}), bf16[2,128,16,128]{3,1,0,2:T(8,128)(2,1)S(1)}, u32[]{:S(2)}, u32[]{:S(2)}) async-start(bf16[2,128,16,128]{3,1,0,2:T(8,128)(2,1)} %bitcast.25), calls=%async_computation.1 | async-start | bytes 2097152 | tf_op jit(solution)/shard_map/all_to_all | solution.py:94
  19.7 60.4 %copy-start.5 = (s32[2]{0:T(128)S(1)}, s32[2]{0:T(128)}, u32[]{:S(2)}) copy-start(s32[2]{0:T(128)} %param.18) | copy-start | bytes 28
  47.3 31.5 %all-to-all-start = ((bf16[2,128,16,128]{3,1,0,2:T(8,128)(2,1)}), bf16[2,128,16,128]{3,1,0,2:T(8,128)(2,1)}, u32[]{:S(2)}, u32[]{:S(2)}) async-start(bf16[2,128,16,128]{3,1,0,2:T(8,128)(2,1)} %bitcast.20), calls=%async_computation | async-start | bytes 2097152 | tf_op jit(solution)/shard_map/all_to_all | solution.py:95
  52.3 144.6 %all-gather.2.cloned.1.call-start = ((), (), s32[]{:S(2)}) async-start(), calls=%async_computation.3 | async-start | bytes 8650752 | tf_op jit(solution)/shard_map/all_gather | solution.py:113
  80.1 16.0 %copy-start.3 = (s32[64]{0:T(128)S(1)}, s32[64]{0:T(128)}, u32[]{:S(2)}) copy-start(s32[64]{0:T(128)} %param.21) | copy-start | bytes 772
  80.1 16.0 %copy-start.4 = (s32[64]{0:T(128)S(1)}, s32[64]{0:T(128)}, u32[]{:S(2)}) copy-start(s32[64]{0:T(128)} %param.20) | copy-start | bytes 772
  96.0 193.2 %reduce-scatter.2.cloned.1.call-start = ((), (), s32[]{:S(2)}) async-start(), calls=%async_computation.4 | async-start | bytes 3342336 | tf_op jit(solution)/shard_map/reduce_scatter | solution.py:118
Sparse Core Ops, SparseCore 0:
  96.1 100.6 all-gather.1
  225.1 64.0 reduce-scatter.1
where the time goes:
time: 297 us; the launch traced here: 296 us
  waiting for transfers between devices  216 us (73%)
  local copies, waits for them, and re-layouts  32.5 us (11%)
  starting transfers between devices  15.5 us (5%)
  between operations  13.6 us (5%)
  matrix products  12.5 us (4%)
  other arithmetic  5.82 us (2%)
    all_gather x1, waiting for transfers between devices, body(): home_all = lax.all_gather(attended_rows, 'dp', axis=0, tiled=True)  99.9 us
    reduce_scatter x1, waiting for transfers between devices, body(): lax.psum_scatter(jnp.dot(picked, out_weight, preferred_element_type=jnp.f...  64.2 us
    all_to_all x1, waiting for transfers between devices, body(): lax.all_to_all(spread(cache_keys), 'tensor', split_axis=2, concat_axis=1,...  26.3 us
    all_to_all x1, waiting for transfers between devices, body(): lax.all_to_all(spread(cache_values), 'tensor', split_axis=2, concat_axis=...  25.4 us
    gather x1, local copies, waits for them, and re-layouts, body(): picked = jnp.take(home_all, request * DRAFT + within, axis=0)  20.4 us
    all_to_all x1, starting transfers between devices, body(): lax.all_to_all(spread(cache_keys), 'tensor', split_axis=2, concat_axis=1,...  10.4 us
    dot_general x1, matrix products, body(): jnp.dot(picked, out_weight, preferred_element_type=jnp.float32)  7.65 us
  transfers between devices with their start and end apart: 4, of which 4 were waited for; matrix products, arithmetic and copies ran while one was open for 1% of the time, Pallas kernels for 0%

commit v1 on v0

--- a/solution.py
+++ b/solution.py
@@ -1,3 +1,4 @@
+import functools
 import jax
 import jax.numpy as jnp
 from jax import lax
@@ -10,6 +11,22 @@
 GROUP_REQ = 2
 PACK = 96
 NEG_FILL = -1e30
+
+
+def field_lay(tile_in, a_name):
+    last = jnp.concatenate(
+        lax.all_to_all(
+            jnp.stack([tile_in] * lax.psum(1, axis_name=a_name)),
+            axis_name=a_name,
+            split_axis=0,
+            concat_axis=0,
+        ),
+        axis=0,
+    )
+    return last
+
+
+play_flows = functools.partial(field_lay, a_name="dp")
 
 
 def packed_sources(row_ids, draft_lengths, dest_group, dest_offset):
@@ -110,7 +127,7 @@
     width_local = local_heads * HEAD_DIM
     attended_rows = attended.reshape(GROUP_REQ * DRAFT, width_local)
     target_rows = PACK * data_count // tensor_count
-    home_all = lax.all_gather(attended_rows, "dp", axis=0, tiled=True)
+    home_all = play_flows(attended_rows)
     row_ids = jnp.arange(lax.axis_size("tensor") * target_rows, dtype=jnp.int32)
     request, within, is_live = packed_sources(row_ids, draft_lengths, dest_group, dest_offset)
     picked = jnp.take(home_all, request * DRAFT + within, axis=0)

time: 297 us -> 408 us (1.37)
  waiting for transfers between devices: 216 us -> 312 us
  starting transfers between devices: 15.5 us -> 25.7 us
  local copies, waits for them, and re-layouts: 32.5 us -> 36.8 us
    all_to_all x0 -> x1, waiting for transfers between devices: none -> 194 us  [field_lay(): lax.all_to_all(jnp.stack([tile_in] * lax.psum(1, axis_name=a_name)), axis...]
    all_gather x1 -> x0, waiting for transfers between devices: 99.9 us -> none  [body(): home_all = lax.all_gather(attended_rows, 'dp', axis=0, tiled=True)]
    all_to_all x0 -> x1, starting transfers between devices: none -> 10.3 us  [field_lay(): lax.all_to_all(jnp.stack([tile_in] * lax.psum(1, axis_name=a_name)), axis...]
    all_to_all x1, starting transfers between devices: 10.4 us -> 4.93 us  [body(): lax.all_to_all(spread(cache_keys), 'tensor', split_axis=2, concat_axis=1,...]
    all_to_all x1, starting transfers between devices: 4.98 us -> 10.4 us  [body(): lax.all_to_all(spread(cache_values), 'tensor', split_axis=2, concat_axis=...]
    another operation x0 -> x1, local copies, waits for them, and re-layouts: none -> 4.28 us  [field_lay(): jnp.stack([tile_in] * lax.psum(1, axis_name=a_name))]
    reduce_scatter x1, waiting for transfers between devices: 64.2 us -> 68.4 us  [body(): lax.psum_scatter(jnp.dot(picked, out_weight, preferred_element_type=jnp.f...]
where the time goes in v1:
time: 408 us; the launch traced here: 407 us
  waiting for transfers between devices  312 us (76%)
  local copies, waits for them, and re-layouts  36.8 us (9%)
  starting transfers between devices  25.7 us (6%)
  between operations  13.6 us (3%)
  matrix products  12.5 us (3%)
  other arithmetic  5.83 us (1%)
    all_to_all x1, waiting for transfers between devices, field_lay(): lax.all_to_all(jnp.stack([tile_in] * lax.psum(1, axis_name=a_name)), axis...  194 us
    reduce_scatter x1, waiting for transfers between devices, body(): lax.psum_scatter(jnp.dot(picked, out_weight, preferred_element_type=jnp.f...  68.4 us
    all_to_all x1, waiting for transfers between devices, body(): lax.all_to_all(spread(cache_values), 'tensor', split_axis=2, concat_axis=...  26.3 us
    all_to_all x1, waiting for transfers between devices, body(): lax.all_to_all(spread(cache_keys), 'tensor', split_axis=2, concat_axis=1,...  23.5 us
    gather x1, local copies, waits for them, and re-layouts, body(): picked = jnp.take(home_all, request * DRAFT + within, axis=0)  20.4 us
    all_to_all x1, starting transfers between devices, body(): lax.all_to_all(spread(cache_values), 'tensor', split_axis=2, concat_axis=...  10.4 us
    all_to_all x1, starting transfers between devices, field_lay(): lax.all_to_all(jnp.stack([tile_in] * lax.psum(1, axis_name=a_name)), axis...  10.3 us
  transfers between devices with their start and end apart: 4, of which 4 were waited for; matrix products, arithmetic and copies ran while one was open for 1% of the time, Pallas kernels for 0%

profile of v1, /device:TPU:8, one launch (start us, length us, event | category | flops | bytes accessed | tf_op | source)
XLA Modules:
  0.0 407.1 jit_solution(17798751463874585295)
XLA Ops:
  6.5 1.3 copy_bitcast_fusion.4
  7.8 1.2 broadcast_in_dim.101
  9.1 10.4 %all-to-all-start = ((bf16[2,128,16,128]{3,1,0,2:T(8,128)(2,1)}), bf16[2,128,16,128]{3,1,0,2:T(8,128)(2,1)S(1)}, u32[]{:S(2)}, u32[]{:S(2)}) async-start(bf16[2,128,16,128]{3,1,0,2:T(8,128)(2,1)} %bitcast.20), calls=%async_computation | async-start | bytes 2097152 | tf_op jit(solution)/shard_map/all_to_all | solution.py:112
  19.7 26.3 %all-to-all-done = bf16[2,128,16,128]{3,1,0,2:T(8,128)(2,1)S(1)} async-done(((bf16[2,128,16,128]{3,1,0,2:T(8,128)(2,1)}), bf16[2,128,16,128]{3,1,0,2:T(8,128)(2,1)S(1)}, u32[]{:S(2)}, u32[]{:S(2)}) %all-to-all-start) | async-done | bytes 1048608 | tf_op jit(solution)/shard_map/all_to_all | solution.py:112
  46.0 1.3 broadcast_in_dim.102
  47.3 4.9 %all-to-all-start.1 = ((bf16[2,128,16,128]{3,1,0,2:T(8,128)(2,1)}), bf16[2,128,16,128]{3,1,0,2:T(8,128)(2,1)S(1)}, u32[]{:S(2)}, u32[]{:S(2)}) async-start(bf16[2,128,16,128]{3,1,0,2:T(8,128)(2,1)} %bitcast.163), calls=%async_computation.1 | async-start | bytes 2097152 | tf_op jit(solution)/shard_map/all_to_all | solution.py:111
  52.2 1.0 copy.48
  53.3 0.8 constant_dynamic-slice_fusion.1
  54.1 1.1 copy.35
  55.2 23.5 %all-to-all-done.1 = bf16[2,128,16,128]{3,1,0,2:T(8,128)(2,1)S(1)} async-done(((bf16[2,128,16,128]{3,1,0,2:T(8,128)(2,1)}), bf16[2,128,16,128]{3,1,0,2:T(8,128)(2,1)S(1)}, u32[]{:S(2)}, u32[]{:S(2)}) %all-to-all-start.1) | async-done | bytes 1048608 | tf_op jit(solution)/shard_map/all_to_all | solution.py:111
  78.8 14.2 %while.10 = (s32[]{:T(128)}, bf16[2,64,1,8,128]{4,3,1,0,2:T(8,128)(2,1)}, s32[2]{0:T(128)S(1)}, bf16[2,2048,1,128]{3,1,2,0:T(8,128)(2,1)}, s32[2]{0:T(128)S(1)},...) while((s32[]{:T(128)}, ...), condition=%wide.region_8.9_spmd, body=%wide.region_3.8_spmd.sunk | while | flops 566699072 | bytes 19887412 | solution.py:123
  80.2 0.9 bitcast_reduce_fusion.2
  82.9 1.0 fusion.71
  83.8 1.1 fusion.73
  87.3 0.9 bitcast_reduce_fusion.2
  90.0 1.0 fusion.71
  90.9 1.1 fusion.73
  93.0 1.0 copy.61
  94.0 4.3 %stack.3 = bf16[32,128,1024]{2,1,0:T(8,128)(2,1)} broadcast(bf16[128,1024]{1,0:T(8,128)(2,1)S(1)} %bitcast.165), dimensions={1,2} | broadcast | bytes 8650752 | tf_op jit(solution)/shard_map/stack | solution.py:19
  98.3 10.3 %all-to-all-start.2 = ((bf16[32,128,1024]{2,1,0:T(8,128)(2,1)}), bf16[32,128,1024]{2,1,0:T(8,128)(2,1)}, u32[]{:S(2)}, u32[]{:S(2)}) async-start(bf16[32,128,1024]{2,1,0:T(8,128)(2,1)} %stack.3), calls=%async_computation.2 | async-start | bytes 16777216 | tf_op jit(solution)/shard_map/all_to_all | solution.py:18
  109.6 194.1 %all-to-all-done.2 = bf16[32,128,1024]{2,1,0:T(8,128)(2,1)} async-done(((bf16[32,128,1024]{2,1,0:T(8,128)(2,1)}), bf16[32,128,1024]{2,1,0:T(8,128)(2,1)}, u32[]{:S(2)}, u32[]{:S(2)}) %all-to-all-start.2) | async-done | bytes 8388640 | tf_op jit(solution)/shard_map/all_to_all | solution.py:18
  303.8 20.4 %gather_fusion = bf16[3072,1024]{1,0:T(8,128)(2,1)} fusion(bf16[4096,1024]{1,0:T(8,128)(2,1)} %bitcast.32, s32[3072]{0:T(1024)S(1)} %broadcast_clamp_fusion), kind=kCustom, calls=%fused_computation | custom fusion | bytes 12595200 | tf_op jit(solution)/shard_map/jit(_take)/gather | solution.py:133
  324.2 7.6 %fusion.34 = bf16[3072,512]{1,0:T(8,128)(2,1)} fusion(bf16[1024,512]{1,0:T(8,128)(2,1)S(1)} %copy-done, bf16[3072,1024]{1,0:T(8,128)(2,1)} %gather_fusion, pred[3072]{0:T(1024)(128)(4,1)S(1)} %compare_and_fusion.1, pred[3072]{0:T(1024)(128)(4,1)S(1)} %fusion.50), kind=kOutput, calls=%fused_computation.49 | convolution fusion | flops 3229089792 | bytes 10491904 | tf_op jit(solution)/shard_map/dot_general | solution.py:136
  331.8 68.4 %reduce-scatter.2.cloned.1.call-done = bf16[192,512]{1,0:T(8,128)(2,1)} async-done(((bf16[3072,512]{1,0:T(8,128)(2,1)}), bf16[192,512]{1,0:T(8,128)(2,1)}) %reduce-scatter.2.cloned.1.call-update) | async-done | bytes 196624 | tf_op jit(solution)/shard_map/reduce_scatter | solution.py:135
  (54 shorter events, 9.5 us)
Async XLA Ops:
  6.5 317.6 %copy-start = (bf16[1024,512]{1,0:T(8,128)(2,1)S(1)}, bf16[1024,512]{1,0:T(8,128)(2,1)}, u32[]{:S(2)}) copy-start(bf16[1024,512]{1,0:T(8,128)(2,1)} %param.17) | copy-start | bytes 3145732
  6.5 13.0 %copy-start.2 = (bf16[2,128,1024]{2,1,0:T(8,128)(2,1)S(1)}, bf16[2,128,1024]{2,1,0:T(8,128)(2,1)}, u32[]{:S(2)}) copy-start(bf16[2,128,1024]{2,1,0:T(8,128)(2,1)} %param.15) | copy-start | bytes 1572868
  7.8 45.4 %copy-start.6 = (s32[64]{0:T(128)S(1)}, s32[64]{0:T(128)}, u32[]{:S(2)}) copy-start(s32[64]{0:T(128)} %param.19) | copy-start | bytes 772
  9.1 36.9 %all-to-all-start = ((bf16[2,128,16,128]{3,1,0,2:T(8,128)(2,1)}), bf16[2,128,16,128]{3,1,0,2:T(8,128)(2,1)S(1)}, u32[]{:S(2)}, u32[]{:S(2)}) async-start(bf16[2,128,16,128]{3,1,0,2:T(8,128)(2,1)} %bitcast.20), calls=%async_computation | async-start | bytes 2097152 | tf_op jit(solution)/shard_map/all_to_all | solution.py:112
  19.6 59.2 %copy-start.5 = (s32[2]{0:T(128)S(1)}, s32[2]{0:T(128)}, u32[]{:S(2)}) copy-start(s32[2]{0:T(128)} %param.18) | copy-start | bytes 28
  47.3 31.4 %all-to-all-start.1 = ((bf16[2,128,16,128]{3,1,0,2:T(8,128)(2,1)}), bf16[2,128,16,128]{3,1,0,2:T(8,128)(2,1)S(1)}, u32[]{:S(2)}, u32[]{:S(2)}) async-start(bf16[2,128,16,128]{3,1,0,2:T(8,128)(2,1)} %bitcast.163), calls=%async_computation.1 | async-start | bytes 2097152 | tf_op jit(solution)/shard_map/all_to_all | solution.py:111
  80.2 3.6 copy-start.1
  87.3 3.6 copy-start.1
  98.3 10.4 %copy-start.3 = (s32[64]{0:T(128)S(1)}, s32[64]{0:T(128)}, u32[]{:S(2)}) copy-start(s32[64]{0:T(128)} %param.21) | copy-start | bytes 772
  98.3 10.5 %copy-start.4 = (s32[64]{0:T(128)S(1)}, s32[64]{0:T(128)}, u32[]{:S(2)}) copy-start(s32[64]{0:T(128)} %param.20) | copy-start | bytes 772
  98.3 205.5 %all-to-all-start.2 = ((bf16[32,128,1024]{2,1,0:T(8,128)(2,1)}), bf16[32,128,1024]{2,1,0:T(8,128)(2,1)}, u32[]{:S(2)}, u32[]{:S(2)}) async-start(bf16[32,128,1024]{2,1,0:T(8,128)(2,1)} %stack.3), calls=%async_computation.2 | async-start | bytes 16777216 | tf_op jit(solution)/shard_map/all_to_all | solution.py:18
  108.7 291.6 %reduce-scatter.2.cloned.1.call-start = ((), (), s32[]{:S(2)}) async-start(), calls=%async_computation.4 | async-start | bytes 3342336 | tf_op jit(solution)/shard_map/reduce_scatter | solution.py:135
Sparse Core Ops, SparseCore 0:
  332.0 68.2 reduce-scatter.1
